TPU v7x, 128 devices: a whole 4x4x4 slice. The times are simulated.
128 devices in a mesh: batch: 1, t: 128 (over z, y, x, core).
Axes of the slice: x: 4, y: 4, z: 4, core: 2. Of those that a mesh axis runs over, the one named last changes fastest.
Arguments:
- z: bfloat16 [256, 16, 96, 128], P(('batch', 't'))
- w: bfloat16 [5, 3, 3, 3, 128, 128], replicated
- b: float32 [5, 128], replicated
- gamma: float32 [4, 128], replicated
- beta: float32 [4, 128], replicated
Outputs:
- output: bfloat16 [512, 32, 192, 128], P(('batch', 't'))
All inputs are finite; a program needn't handle non-finite values.
Results may differ from a plain program's by a relative error of at most 0.0145726.
Values are sent between devices in bfloat16 or wider.
A program may use at most 1 GiB of HBM per device.

v0:
```python
import jax
import jax.numpy as jnp
from jax import lax
from jax.experimental import pallas as pl
from jax.experimental.pallas import tpu as pltpu
from jax.sharding import PartitionSpec as P

F32, BF = jnp.float32, jnp.bfloat16
EPS = 1e-6
C = 128
C2, C3, C4 = 2 * C, 3 * C, 4 * C
ALL, LOW, HIGH, MID = slice(0, C2), slice(0, C), slice(C, C2), slice(C, C3)
TAPS = range(3)
PAIR = range(2)
MESH = pl.DeviceIdType.MESH
R = 8


def dup(v):
    return jnp.concatenate([v, v], axis=1)


def dot(a, b):
    return jnp.dot(a, b, preferred_element_type=F32)


def plus(a, b):
    return b if a is None else a + b


def group_sum(s):
    lane = lax.broadcasted_iota(jnp.int32, s.shape, 1) % 4
    out = s
    for k in (1, 2, 3):
        out = out + jnp.where(lane + k < 4, pltpu.roll(s, C - k, 1), pltpu.roll(s, 4 - k, 1))
    return out


def norm_rows(s, cnt):
    s = group_sum(s)
    mean = s[0:1] / cnt
    return mean, lax.rsqrt(s[1:2] / cnt - mean * mean + EPS)


def act(x, mean, inv, g, be):
    v = (((x.astype(F32) - mean) * inv) * g + be).astype(BF).astype(F32)
    return v * jax.nn.sigmoid(v)


def shift(v, by):
    n = v.shape[0]
    row = lax.broadcasted_iota(jnp.int32, v.shape, 0)
    return jnp.where(row == (0 if by > 0 else n - 1), 0.0, pltpu.roll(v, by % n, 0))


def stats_of(h):
    hf = h.astype(F32)
    return jnp.sum(hf, axis=0, keepdims=True), jnp.sum(hf * hf, axis=0, keepdims=True)


class Net:
    def __init__(self, n, slots0, slots1, cur, ssem, rsem):
        self.n, self.slots, self.cur, self.ssem, self.rsem = n, (slots0, slots1), cur, ssem, rsem
        self.groups = (8, n // 8)
        self.strides = (1, 8)
        self.me = lax.axis_index('t')
        self.next = lax.rem(self.me + 1, n)
        self.prev = lax.rem(self.me + n - 1, n)

    @staticmethod
    def scratch(n, nsum):
        dma = pltpu.SemaphoreType.DMA((nsum, 2))
        return [pltpu.VMEM((nsum, g, 2, C), F32) for g in (8, n // 8)] + [pltpu.VMEM((nsum, 2, 2, C), F32), dma, dma]

    def peer(self, k, i):
        g, st = self.groups[k], self.strides[k]
        d = lax.rem(lax.div(self.me, st), g)
        return self.me + (lax.rem(d + i, g) - d) * st, d

    def greet(self):
        bar = pltpu.get_barrier_semaphore()
        peers = [self.peer(k, i)[0] for k in PAIR for i in range(1, self.groups[k])]
        for d in peers + [self.next, self.prev]:
            pl.semaphore_signal(bar, inc=1, device_id={'t': d}, device_id_type=MESH)

    def met(self):
        pl.semaphore_wait(pltpu.get_barrier_semaphore(), sum(self.groups))

    def send(self, src, dst, ssem, rsem):
        cp = pltpu.make_async_remote_copy(src, dst, ssem, rsem, device_id={'t': self.next}, device_id_type=MESH)
        cp.start()
        return cp

    def total(self, j, v, *after):
        for k in PAIR:
            g = self.groups[k]
            buf = self.slots[k]
            d = self.peer(k, 0)[1]
            self.cur[j, k] = v
            buf[j, pl.ds(d, 1)] = v[None]
            for i in range(1, g):
                pltpu.make_async_remote_copy(self.cur.at[j, k], buf.at[j, d], self.ssem.at[j, k], self.rsem.at[j, k], device_id={'t': self.peer(k, i)[0]}, device_id_type=MESH).start()
            if k == 0:
                for job in after:
                    job()
            w = buf.at[j, pl.ds(0, g - 1)]
            pltpu.make_async_copy(w, w, self.rsem.at[j, k]).wait()
            v = jnp.sum(buf[j], axis=0)
        return v

    def close(self, j):
        for k in PAIR:
            w = self.slots[k].at[j, pl.ds(0, self.groups[k] - 1)]
            pltpu.make_async_copy(w, w, self.ssem.at[j, k]).wait()


def section(z, w, b, gamma, beta, nt, cnt1, cnt2):
    n, hh, ww, _ = z.shape
    wp = ww + 16
    half = hh // 2
    h2 = 2 * hh
    own = 2 * n
    nu = own + 2
    SUB = 2

    def kern(z_ref, w_ref, b_ref, g_ref, be_ref, y_ref, wv, h, hal, x, xhal, U, H, Hh, st, wsem, hs, hr, bs, br, *net):
        nw = Net(nt, *net)
        nw.greet()
        wcp = [pltpu.make_async_copy(w_ref.at[pl.ds(27 * i, 27)], wv.at[i], wsem.at[i]) for i in range(5)]
        for cp in wcp:
            cp.start()
        first = nw.me == 0
        zero = jnp.zeros((1, C), F32)
        zcc = jnp.zeros((C, C), BF)
        sends = []

        def keep(t):
            st[0:1] = t[0]
            st[1:2] = t[1]
            return st[...]

        def phase_a(A, W, X, Wpp, Wpc, Wcp, Wcc, PP, PC, CP, CC, Q):
            def zbody(i, c):
                a, d = stats_of(z_ref[i // hh, i % hh])
                return c[0] + a, c[1] + d
            zs = lax.fori_loop(0, n * hh, zbody, (zero, zero))

            def build(i):
                wcp[i].wait()
                for q in range(4):
                    for di in TAPS:
                        for dj in TAPS:
                            t = di * 3 + dj
                            rows = pl.ds(dj * C, C)
                            W[q * 3 + di, rows, LOW] = wv[i, q * 9 + t] if q < 3 else zcc
                            W[q * 3 + di, rows, HIGH] = wv[i, (q - 1) * 9 + t] if q > 0 else zcc

            def halo(k, src, dst):
                sends.append(nw.send(src, dst, hs.at[k], hr.at[k]))

            def conv(i, src, mine, tot, emit):
                mean, inv = norm_rows(tot, cnt1)
                gg, bb = g_ref[i:i + 1], be_ref[i:i + 1]

                def fill(q):
                    A[q, 0] = jnp.zeros((ww, C3), BF)
                    A[q, hh + 1] = jnp.zeros((ww, C3), BF)

                    def arow(r, c):
                        v = mine[q - 2, r] if q >= 2 else jnp.where(first, mine[0, r], src[q, r])
                        v = act(v, mean, inv, gg, bb)
                        A[q, r + 1, :, HIGH] = v.astype(BF)
                        A[q, r + 1, :, LOW] = shift(v, 1).astype(BF)
                        A[q, r + 1, :, C2:C3] = shift(v, -1).astype(BF)
                        return c
                    lax.fori_loop(0, hh, arow, 0, unroll=2)
                fill(2)
                fill(3)
                sends[-1].wait_recv()
                fill(0)
                fill(1)
                bias = dup(b_ref[i:i + 1])
                for rc in range(hh // R):
                    parts = [A[q, pl.ds(rc * R + di, R)].reshape(R * ww, C3) for q in range(4) for di in TAPS]
                    acc = dot(jnp.concatenate(parts, axis=1), W[...].reshape(12 * C3, C2))
                    emit(pl.ds(rc * R, R), (acc + bias).astype(BF), rc)

            nw.met()
            tot = nw.total(0, keep(zs), lambda: halo(0, z_ref, hal.at[0]), lambda: build(0))
            part = []

            def emit0(rows, v, rc):
                for f in PAIR:
                    h[f, rows] = v[:, f * C:(f + 1) * C].reshape(R, ww, C)
                part.append([a[:, LOW] + a[:, HIGH] for a in stats_of(v)])
            conv(0, hal.at[0], z_ref, tot, emit0)
            tot = nw.total(1, keep([sum(p) for p in zip(*part)]), lambda: halo(1, h, hal.at[1]), lambda: build(1))

            def emit1(rows, v, rc):
                for f in PAIR:
                    x[f, rows] = (z_ref[f, rows].astype(F32) + v[:, f * C:(f + 1) * C].reshape(R, ww, C).astype(F32)).astype(BF)
                halo(2 + rc, x.at[:, rows], xhal.at[:, rows])
            conv(1, hal.at[1], h, tot, emit1)

            wcp[2].wait()

            def put(Wd, k, t):
                for ti in PAIR:
                    Wd[ti, pl.ds(k * C, C), LOW] = wv[2, 18 * ti + t]
                    Wd[ti, pl.ds(k * C, C), HIGH] = wv[2, 9 + t] if ti else zcc
            for Wd, ts in ((Wpp, (0, 2, 6, 8)), (Wpc, (1, 7)), (Wcp, (3, 5)), (Wcc, (4,))):
                for k, t in enumerate(ts):
                    put(Wd, k, t)
            bias = b_ref[2:3]

            def place(q):
                X[q, 0] = jnp.zeros((wp, C2), BF)
                X[q, hh + 1] = jnp.zeros((wp, C2), BF)

                def xrow(r, c):
                    v = x[q - 2, r] if q >= 2 else jnp.where(first, x[0, r], xhal[q, r])
                    X[q, r + 1, 0:ww, HIGH] = v
                    X[q, r + 1, ww:wp, HIGH] = jnp.zeros((16, C), BF)
                    vf = v.astype(F32)
                    X[q, r + 1, 0:ww, LOW] = shift(vf, 1).astype(BF)
                    tail = jnp.where(lax.broadcasted_iota(jnp.int32, (16, C), 0) == 0, vf[ww - 1:ww], 0.0)
                    X[q, r + 1, ww:wp, LOW] = tail.astype(BF)
                    return c
                lax.fori_loop(0, hh, xrow, 0, unroll=2)

            def frame(q, full):
                frames = (q - 1, q) if full else (q,)

                def part_dot(D, Wd, rows, r0, nr, cols):
                    wd = ww if cols else wp
                    parts = [X[f, pl.ds(r0 + dr, nr), 0:wd, cols:C2].reshape(nr * wd, C2 - cols) for f in frames for dr in rows]
                    wt = Wd[...].reshape(2 * Wd.shape[1], C2) if full else Wd[1]
                    D[pl.ds(r0, nr)] = dot(jnp.concatenate(parts, axis=1), wt).reshape(nr, wd, C2)

                for r0, nr in ((0, half), (half, half + 1)):
                    part_dot(PP, Wpp, (0, 1), r0, nr, 0)
                    part_dot(PC, Wpc, (0, 1), r0, nr, C)
                for r0 in (0, half):
                    part_dot(CP, Wcp, (1,), r0, half, 0)
                    part_dot(CC, Wcc, (1,), r0, half, C)
                lanes = ALL if full else HIGH

                def comb(i, c):
                    cp, cc = CP[i, :, lanes], CC[i, :, lanes]
                    c = list(c)
                    for pr in PAIR:
                        fp = PP[i + pr, :, lanes] + cp
                        fc = PC[i + pr, :, lanes] + cc
                        for pc in PAIR:
                            v = (pltpu.roll(fp, wp - 1, 0) if pc else fp)[0:ww] + fc
                            if full:
                                for e, t in enumerate((Q[pr, pc, i], v[:, HIGH])):
                                    o = ((v[:, LOW] + t) + bias).astype(BF)
                                    U[2 * q - 2 + e, 2 * i + pr, :, pc * C:(pc + 1) * C] = o
                                    a, d = stats_of(o)
                                    c[2 * e], c[2 * e + 1] = c[2 * e] + a, c[2 * e + 1] + d
                            Q[pr, pc, i] = v[:, HIGH] if full else v
                    return tuple(c)
                c = lax.fori_loop(0, hh, comb, (zero,) * 4)
                drop = jnp.logical_and(first, q == 2)
                return [jnp.where(drop, 0.0, c[k]) + c[2 + k] for k in PAIR]

            place(2)
            place(3)
            frame(2, False)
            sums = frame(3, True)
            for cp in sends[2:]:
                cp.wait_recv()
            place(0)
            place(1)
            frame(0, False)
            own0 = lax.fori_loop(1, 3, lambda q, c: tuple(frame(q, True)), (zero, zero))
            keep([a + d for a, d in zip(sums, own0)])
            for cp in sends:
                cp.wait_send()
            for j in PAIR:
                nw.close(j)

        def phase_b(A0, A1, A2, A3, A4, A5, W, WE, WO, T, Y, ysem):
            A = (A0, A1, A2, A3, A4, A5)

            def build(i):
                wcp[i].wait()
                for t in range(9):
                    for a in PAIR:
                        for o in PAIR:
                            W[t, a * C:(a + 1) * C, o * C:(o + 1) * C] = wv[i, t * 3 + a - o + 1]
                for k in TAPS:
                    for p in range(4):
                        for o in PAIR:
                            t = (k * 3 + p - o) * 3
                            for Wx, dj in ((WE, 0), (WO, 2)):
                                Wx[k * 4 + p, :, o * C:(o + 1) * C] = wv[i, t + dj] if 0 <= p - o <= 2 else zcc

            def prep():
                build(3)
                for a in A:
                    a[0] = jnp.zeros((ww, C4), BF)
                    a[h2 + 1] = jnp.zeros((ww, C4), BF)

            def filler(i, tot, src):
                mean, inv = norm_rows(tot, cnt2)
                mean, inv, gg, bb = dup(mean), dup(inv), dup(g_ref[i - 1:i]), dup(be_ref[i - 1:i])

                def row(k, r):
                    v = act(src(k, r), mean, inv, gg, bb)
                    a = A[k]
                    a[r + 1, :, MID] = v.astype(BF)
                    a[r + 1, :, LOW] = shift(v[:, HIGH], 1).astype(BF)
                    a[r + 1, :, C3:C4] = shift(v[:, LOW], -1).astype(BF)
                return row

            def fill(row, ks):
                def body(r, c):
                    for k in ks:
                        row(k, r)
                    return c
                lax.fori_loop(0, h2, body, 0)

            def conv(i, f, row, ks, emit, done):
                bias = b_ref[i:i + 1]

                def trip(j, c):
                    for s in range(SUB):
                        r0 = j * (SUB * R) + s * R
                        todo = [(k, r0 + q) for q in range(R) for k in ks]
                        step = -(-len(todo) // 15)

                        def some():
                            for _ in range(step):
                                if todo:
                                    row(*todo.pop(0))
                        acc = None
                        left = [None, None]
                        for k in TAPS:
                            a = A[f + k]
                            for di in TAPS:
                                acc = plus(acc, dot(a[pl.ds(r0 + di, R), :, MID].reshape(R * ww, C2), W[k * 3 + di]))
                                some()
                            for e, (Wx, l0) in enumerate(((WE, 0), (WO, C3))):
                                lhs = [jnp.concatenate([a[r0 + p + q, :, l0:l0 + C] for q in range(0, R, 2)], axis=0) for p in range(4)]
                                left[e] = plus(left[e], dot(jnp.concatenate(lhs, axis=1), Wx[k * 4:k * 4 + 4].reshape(C4, C2)))
                                some()
                        while todo:
                            some()
                        for q in range(R):
                            m = acc[q * ww:(q + 1) * ww]
                            lr = slice(q // 2 * ww, (q // 2 + 1) * ww)
                            lc = slice(q % 2 * C, (q % 2 + 1) * C)
                            c = emit(r0 + q, q, [(m[:, hf] + left[e][lr, lc] + bias).astype(BF) for e, hf in enumerate((LOW, HIGH))], c)
                    return done(j, c)
                return lax.fori_loop(0, h2 // (SUB * R), trip, (zero, zero))

            def conv3(f, row, ks, send=None):
                def emit(r, q, v, c):
                    H[f, r, :, LOW], H[f, r, :, HIGH] = v
                    v = [a.astype(F32) for a in v]
                    return c[0] + jnp.sum(v[0] + v[1], axis=0, keepdims=True), c[1] + jnp.sum(v[0] * v[0] + v[1] * v[1], axis=0, keepdims=True)

                def done(j, c):
                    if send is not None:
                        send(pl.ds(j * (SUB * R), SUB * R))
                    return c
                return conv(3, f, row, ks, emit, done)

            def conv4(f, row, ks):
                slot = f % 2

                def emit(r, q, v, c):
                    for e, hf in enumerate((LOW, HIGH)):
                        T[pl.ds(q * 2 * ww + e, ww, stride=2), :] = U[f + 2, r, :, hf].astype(F32) + v[e].astype(F32)
                    Y[slot, r] = T[q * 2 * ww:(q + 1) * 2 * ww].astype(BF)
                    return c

                def done(j, c):
                    rows = pl.ds(j * (SUB * R), SUB * R)
                    pltpu.make_async_copy(Y.at[slot, rows], y_ref.at[f, rows], ysem.at[slot]).start()
                    return c
                conv(4, f, row, ks, emit, done)
                return pltpu.make_async_copy(Y.at[slot], y_ref.at[f], ysem.at[slot])

            row = filler(3, nw.total(2, st[...], prep), lambda k, r: U[k, r])
            fill(row, (3, 4, 5))
            big = [pltpu.make_async_remote_copy(H.at[f], Hh.at[f - 2], bs.at[f - 2], br.at[f - 2], device_id={'t': nw.next}, device_id_type=MESH) for f in (2, 3)]
            sums = [conv3(3, row, (2,), lambda rows: nw.send(H.at[3, rows], Hh.at[1, rows], bs.at[1], br.at[1]))]
            sums.append(conv3(2, row, (1,)))
            sums.append(conv3(1, row, (0,)))
            sums.append([jnp.where(first, 0.0, a) for a in conv3(0, row, ())])
            tot = nw.total(3, keep([sum(p) for p in zip(*sums)]), lambda: build(4))
            big[0].start()

            row = filler(4, tot, lambda k, r: H[k - 2, r] if k >= 2 else jnp.where(first, H[0, r], Hh[k, r]))
            fill(row, (3, 4, 5))
            y3 = conv4(3, row, (2,))
            big[1].wait_recv()
            y2 = conv4(2, row, (1,))
            y3.wait()
            y1 = conv4(1, row, ())
            y2.wait()
            big[0].wait_recv()
            fill(row, (0,))
            y0 = conv4(0, row, ())
            for cp in big:
                cp.wait_send()
            for j in (2, 3):
                nw.close(j)
            y0.wait()
            y1.wait()

        V = pltpu.VMEM
        pl.run_scoped(
            phase_a, V((4, hh + 2, ww, C3), BF), V((12, C3, C2), BF), V((4, hh + 2, wp, C2), BF),
            *[V((2, k * C, C2), BF) for k in (4, 2, 2, 1)],
            V((hh + 1, wp, C2), F32), V((hh + 1, ww, C2), F32), V((hh, wp, C2), F32), V((hh, ww, C2), F32), V((2, 2, hh, ww, C), F32))
        pl.run_scoped(
            phase_b, *[V((h2 + 2, ww, C4), BF) for _ in range(nu)], V((9, C2, C2), BF), V((12, C, C2), BF), V((12, C, C2), BF),
            V((2 * R * ww, C), F32), V((2, h2, 2 * ww, C), BF), pltpu.SemaphoreType.DMA((2,)))

    vm = pl.BlockSpec(memory_space=pltpu.VMEM)
    hbm = pl.BlockSpec(memory_space=pl.ANY)
    V, D = pltpu.VMEM, pltpu.SemaphoreType.DMA
    nh = 2 + hh // R
    wide = (h2, ww, C2)
    return pl.pallas_call(
        kern, in_specs=[vm, hbm, vm, vm, vm], out_specs=hbm,
        out_shape=jax.ShapeDtypeStruct((own, h2, 2 * ww, C), BF),
        scratch_shapes=[
            V((5, 27, C, C), BF), V(z.shape, BF), V((2,) + z.shape, BF), V(z.shape, BF), V(z.shape, BF),
            V((nu,) + wide, BF), V((own,) + wide, BF), V((2,) + wide, BF), V((2, C), F32),
            D((5,)), D((nh,)), D((nh,)), D((2,)), D((2,))] + Net.scratch(nt, 4),
        compiler_params=pltpu.CompilerParams(collective_id=0, has_side_effects=True, vmem_limit_bytes=63 * 2**20), name='section')(z, w, b, gamma, beta)


def solution(mesh):
    nt = mesh.shape['t']

    def local(z, w, b, gamma, beta):
        n, hh, ww, c = z.shape
        cnt1 = float(nt * n * hh * ww * 4)
        cnt2 = float((nt * 2 * n - 1) * 4 * hh * ww * 4)
        return section(z, w.reshape(5 * 27, C, C), b, gamma, beta, nt, cnt1, cnt2)

    spec = P(('batch', 't'))
    return jax.shard_map(local, mesh=mesh, in_specs=(spec, P(), P(), P(), P()), out_specs=spec, check_vma=False)
```

profile of v0, /device:TPU:1, one launch (start us, length us, event | category | flops | bytes accessed | tf_op | source)
XLA Modules:
  0.0 159.0 jit_solution(143521120518478775)
XLA Ops:
  0.0 153.1 %section.1 = bf16[4,32,192,128]{3,2,1,0:T(8,128)(2,1)} custom-call(bf16[2,16,96,128]{3,2,1,0:T(8,128)(2,1)} %z_ref.1, bf16[135,128,128]{2,1,0:T(8,128)(2,1)} %bitcast.1, f32[5,128]{1,0:T(8,128)} %b_ref.1, f32[4,128]{1,0:T(4,128)} %g_ref.1, f32[4,128]{1,0:T(4,128)} %be_ref.1), custom_call_target="tpu_custom_call" | custom-call | tf_op jit(solution)/shard_map/section/pallas_call | solution.py:429
  153.1 5.9 %copy.7 = bf16[4,32,192,128]{3,2,1,0:T(8,128)(2,1)} copy(bf16[4,32,192,128]{3,2,1,0:T(8,128)(2,1)} %section.1) | data formatting | bytes 12582912
where the time goes:
time: 159 us
  Pallas kernels  153 us (96%)
  local copies, waits for them, and re-layouts  5.93 us (4%)
    pallas_call x1, Pallas kernels, section(): pl.pallas_call(kern, in_specs=[vm, hbm, vm, vm, vm], out_specs=hbm, out_s...  153 us
    unnamed x1, local copies, waits for them, and re-layouts  5.93 us

commit v1 on v0

--- a/solution.py
+++ b/solution.py
@@ -281,7 +281,7 @@
             for j in PAIR:
                 nw.close(j)
 
-        def phase_b(A0, A1, A2, A3, A4, A5, W, WE, WO, T, Y, ysem):
+        def phase_b(A0, A1, A2, A3, A4, A5, W, WE, WO, T):
             A = (A0, A1, A2, A3, A4, A5)
 
             def build(i):
@@ -369,20 +369,14 @@
                 return conv(3, f, row, ks, emit, done)
 
             def conv4(f, row, ks):
-                slot = f % 2
 
                 def emit(r, q, v, c):
                     for e, hf in enumerate((LOW, HIGH)):
                         T[pl.ds(q * 2 * ww + e, ww, stride=2), :] = U[f + 2, r, :, hf].astype(F32) + v[e].astype(F32)
-                    Y[slot, r] = T[q * 2 * ww:(q + 1) * 2 * ww].astype(BF)
+                    y_ref[f, r] = T[q * 2 * ww:(q + 1) * 2 * ww].astype(BF)
                     return c
 
-                def done(j, c):
-                    rows = pl.ds(j * (SUB * R), SUB * R)
-                    pltpu.make_async_copy(Y.at[slot, rows], y_ref.at[f, rows], ysem.at[slot]).start()
-                    return c
-                conv(4, f, row, ks, emit, done)
-                return pltpu.make_async_copy(Y.at[slot], y_ref.at[f], ysem.at[slot])
+                conv(4, f, row, ks, emit, lambda j, c: c)
 
             row = filler(3, nw.total(2, st[...], prep), lambda k, r: U[k, r])
             fill(row, (3, 4, 5))
@@ -396,21 +390,17 @@
 
             row = filler(4, tot, lambda k, r: H[k - 2, r] if k >= 2 else jnp.where(first, H[0, r], Hh[k, r]))
             fill(row, (3, 4, 5))
-            y3 = conv4(3, row, (2,))
+            conv4(3, row, (2,))
             big[1].wait_recv()
-            y2 = conv4(2, row, (1,))
-            y3.wait()
-            y1 = conv4(1, row, ())
-            y2.wait()
+            conv4(2, row, (1,))
+            conv4(1, row, ())
             big[0].wait_recv()
             fill(row, (0,))
-            y0 = conv4(0, row, ())
+            conv4(0, row, ())
             for cp in big:
                 cp.wait_send()
             for j in (2, 3):
                 nw.close(j)
-            y0.wait()
-            y1.wait()
 
         V = pltpu.VMEM
         pl.run_scoped(
@@ -419,7 +409,7 @@
             V((hh + 1, wp, C2), F32), V((hh + 1, ww, C2), F32), V((hh, wp, C2), F32), V((hh, ww, C2), F32), V((2, 2, hh, ww, C), F32))
         pl.run_scoped(
             phase_b, *[V((h2 + 2, ww, C4), BF) for _ in range(nu)], V((9, C2, C2), BF), V((12, C, C2), BF), V((12, C, C2), BF),
-            V((2 * R * ww, C), F32), V((2, h2, 2 * ww, C), BF), pltpu.SemaphoreType.DMA((2,)))
+            V((2 * R * ww, C), F32))
 
     vm = pl.BlockSpec(memory_space=pltpu.VMEM)
     hbm = pl.BlockSpec(memory_space=pl.ANY)
@@ -427,13 +417,13 @@
     nh = 2 + hh // R
     wide = (h2, ww, C2)
     return pl.pallas_call(
-        kern, in_specs=[vm, hbm, vm, vm, vm], out_specs=hbm,
-        out_shape=jax.ShapeDtypeStruct((own, h2, 2 * ww, C), BF),
+        kern, in_specs=[vm, hbm, vm, vm, vm], out_specs=vm,
+        out_shape=pltpu.VMEM((own, h2, 2 * ww, C), BF),
         scratch_shapes=[
             V((5, 27, C, C), BF), V(z.shape, BF), V((2,) + z.shape, BF), V(z.shape, BF), V(z.shape, BF),
             V((nu,) + wide, BF), V((own,) + wide, BF), V((2,) + wide, BF), V((2, C), F32),
             D((5,)), D((nh,)), D((nh,)), D((2,)), D((2,))] + Net.scratch(nt, 4),
-        compiler_params=pltpu.CompilerParams(collective_id=0, has_side_effects=True, vmem_limit_bytes=63 * 2**20), name='section')(z, w, b, gamma, beta)
+        compiler_params=pltpu.CompilerParams(collective_id=0, has_side_effects=True, vmem_limit_bytes=55 * 2**20), name='section')(z, w, b, gamma, beta)
 
 
 def solution(mesh):

time: 159 us -> 155 us (0.975)
  local copies, waits for them, and re-layouts: 5.93 us -> 2.71 us
    unnamed x1, local copies, waits for them, and re-layouts: 5.93 us -> 2.71 us
where the time goes in v1:
time: 155 us
  Pallas kernels  152 us (98%)
  local copies, waits for them, and re-layouts  2.71 us (2%)
    pallas_call x1, Pallas kernels, section(): pl.pallas_call(kern, in_specs=[vm, hbm, vm, vm, vm], out_specs=vm, out_sh...  152 us

profile of v1, /device:TPU:1, one launch (start us, length us, event | category | flops | bytes accessed | tf_op | source)
XLA Modules:
  0.0 154.8 jit_solution(8700599870175093980)
XLA Ops:
  0.0 152.0 %section.1 = bf16[4,32,192,128]{3,2,1,0:T(8,128)(2,1)S(1)} custom-call(bf16[2,16,96,128]{3,2,1,0:T(8,128)(2,1)} %z_ref.1, bf16[135,128,128]{2,1,0:T(8,128)(2,1)} %bitcast.1, f32[5,128]{1,0:T(8,128)} %b_ref.1, f32[4,128]{1,0:T(4,128)} %g_ref.1, f32[4,128]{1,0:T(4,128)} %be_ref.1), custom_call_target="tpu_custom_call" | custom-call | tf_op jit(solution)/shard_map/section/pallas_call | solution.py:419
  152.1 2.7 %copy.7 = bf16[4,32,192,128]{3,2,1,0:T(8,128)(2,1)} copy(bf16[4,32,192,128]{3,2,1,0:T(8,128)(2,1)S(1)} %section.1) | data formatting | bytes 12582912

commit v2 on v1

--- a/solution.py
+++ b/solution.py
@@ -173,17 +173,22 @@
                         A[q, r + 1, :, LOW] = shift(v, 1).astype(BF)
                         A[q, r + 1, :, C2:C3] = shift(v, -1).astype(BF)
                         return c
-                    lax.fori_loop(0, hh, arow, 0, unroll=2)
+                    lax.fori_loop(0, hh, arow, 0, unroll=4)
+                def taps_of(qs, rc):
+                    parts = [A[q, pl.ds(rc * R + di, R)].reshape(R * ww, C3) for q in qs for di in TAPS]
+                    return dot(jnp.concatenate(parts, axis=1), W[3 * qs[0]:3 * qs[0] + 6].reshape(6 * C3, C2))
                 fill(2)
                 fill(3)
+                for rc in range(hh // R):
+                    CC[pl.ds(rc * R, R)] = taps_of((2, 3), rc).reshape(R, ww, C2)
                 sends[-1].wait_recv()
                 fill(0)
                 fill(1)
                 bias = dup(b_ref[i:i + 1])
                 for rc in range(hh // R):
-                    parts = [A[q, pl.ds(rc * R + di, R)].reshape(R * ww, C3) for q in range(4) for di in TAPS]
-                    acc = dot(jnp.concatenate(parts, axis=1), W[...].reshape(12 * C3, C2))
-                    emit(pl.ds(rc * R, R), (acc + bias).astype(BF), rc)
+                    rows = pl.ds(rc * R, R)
+                    acc = CC[rows].reshape(R * ww, C2) + taps_of((0, 1), rc)
+                    emit(rows, (acc + bias).astype(BF), rc)
 
             nw.met()
             tot = nw.total(0, keep(zs), lambda: halo(0, z_ref, hal.at[0]), lambda: build(0))
@@ -320,7 +325,7 @@
                     for k in ks:
                         row(k, r)
                     return c
-                lax.fori_loop(0, h2, body, 0)
+                lax.fori_loop(0, h2, body, 0, unroll=2)
 
             def conv(i, f, row, ks, emit, done):
                 bias = b_ref[i:i + 1]

time: 155 us -> 154 us (level)
  no operation moved by 1% of the time
where the time goes in v2:
time: 154 us
  Pallas kernels  151 us (98%)
  local copies, waits for them, and re-layouts  2.71 us (2%)
    pallas_call x1, Pallas kernels, section(): pl.pallas_call(kern, in_specs=[vm, hbm, vm, vm, vm], out_specs=vm, out_sh...  151 us

profile of v2, /device:TPU:1, one launch (start us, length us, event | category | flops | bytes accessed | tf_op | source)
XLA Modules:
  0.0 154.1 jit_solution(14998207573999626968)
XLA Ops:
  0.0 151.4 %section.1 = bf16[4,32,192,128]{3,2,1,0:T(8,128)(2,1)S(1)} custom-call(bf16[2,16,96,128]{3,2,1,0:T(8,128)(2,1)} %z_ref.1, bf16[135,128,128]{2,1,0:T(8,128)(2,1)} %bitcast.1, f32[5,128]{1,0:T(8,128)} %b_ref.1, f32[4,128]{1,0:T(4,128)} %g_ref.1, f32[4,128]{1,0:T(4,128)} %be_ref.1), custom_call_target="tpu_custom_call" | custom-call | tf_op jit(solution)/shard_map/section/pallas_call | solution.py:424
  151.4 2.7 %copy.7 = bf16[4,32,192,128]{3,2,1,0:T(8,128)(2,1)} copy(bf16[4,32,192,128]{3,2,1,0:T(8,128)(2,1)S(1)} %section.1) | data formatting | bytes 12582912
